TPU v7x, 32 devices: a whole 2x2x4 slice. The times are simulated.
32 devices in a mesh: dp: 16 (over z, y, x), mp: 2 (over core).
Axes of the slice: x: 2, y: 2, z: 4, core: 2. Of those that a mesh axis runs over, the one named last changes fastest.
Arguments:
- inputs: bfloat16 [2048, 1792], P('dp', 'mp'), may hold values from -6 to 6
- cotangent: bfloat16 [2048, 1792], P('dp', 'mp'), may hold values from -6 to 6
- gate_weight: bfloat16 [9472, 1792], P(('mp', 'dp')), may hold values from -0.125 to 0.125
- up_weight: bfloat16 [9472, 1792], P(('mp', 'dp')), may hold values from -0.125 to 0.125
- down_weight: bfloat16 [9472, 1792], P(('mp', 'dp')), may hold values from -0.0625 to 0.0625
Outputs:
- input_grad: bfloat16 [2048, 1792], P('dp', 'mp')
- gate_grad: bfloat16 [9472, 1792], P(('mp', 'dp'))
All inputs are finite; a program needn't handle non-finite values.
Results may differ from a plain program's by a relative error of at most 0.009.
Values may be sent and summed in bfloat16 or wider, within the bound.
A program may use at most 320 MiB of HBM per device.

v0:
```python
import jax
import jax.numpy as jnp
from jax import lax
from jax.sharding import PartitionSpec as P


def tdot(left, right):
    return lax.dot_general(
        left, right, (((0,), (0,)), ((), ())), preferred_element_type=jnp.float32
    )


def rdot(left, right):
    return lax.dot_general(
        left, right, (((1,), (1,)), ((), ())), preferred_element_type=jnp.float32
    )


def per_device(inputs, cotangent, gate_weight, up_weight, down_weight):

    def tokens(block):
        rows = lax.all_gather(block, "dp", axis=0, tiled=True)
        return lax.all_gather(rows, "mp", axis=1, tiled=True)

    full_in = tokens(inputs)
    full_cot = tokens(cotangent)
    gate = rdot(full_in, gate_weight)
    up = rdot(full_in, up_weight)
    dhidden = rdot(full_cot, down_weight)
    sig = jax.nn.sigmoid(gate)
    act = gate * sig
    dup = (dhidden * act).astype(jnp.bfloat16)
    dgate = (dhidden * up * sig * (1.0 + gate * (1.0 - sig))).astype(jnp.bfloat16)
    partial = jnp.dot(dgate, gate_weight, preferred_element_type=jnp.float32)
    partial = partial + jnp.dot(dup, up_weight, preferred_element_type=jnp.float32)
    partial = lax.psum_scatter(partial.astype(jnp.bfloat16), "mp", scatter_dimension=1, tiled=True)
    input_grad = lax.psum_scatter(partial, "dp", scatter_dimension=0, tiled=True)
    gate_grad = tdot(dgate, full_in).astype(jnp.bfloat16)
    return (input_grad, gate_grad)


def solution(mesh):
    placed = (
        P("dp", "mp"),
        P("dp", "mp"),
        P(("mp", "dp"), None),
        P(("mp", "dp"), None),
        P(("mp", "dp"), None),
    )
    return jax.shard_map(
        per_device,
        mesh=mesh,
        in_specs=placed,
        out_specs=(P("dp", "mp"), P(("mp", "dp"), None)),
        check_vma=False,
    )
```

profile of v0, /device:TPU:0, one launch (start us, length us, event | category | flops | bytes accessed | tf_op | source)
XLA Modules:
  0.0 350.5 jit_solution(10456565937666532263)
XLA Ops:
  7.2 0.0 copy-start
  7.2 0.0 all-gather.5.cloned.1.call-start
  7.2 0.7 all-gather.5.cloned.1.call-update
  7.9 0.0 all-gather.9.cloned.1.call-start
  8.0 0.7 all-gather.9.cloned.1.call-update
  8.7 0.0 all-gather.7.cloned.1.call-start
  8.7 76.4 %all-gather.5.cloned.1.call-done = bf16[2048,896]{1,0:T(8,128)(2,1)} async-done(((bf16[128,896]{1,0:T(8,128)(2,1)}), bf16[2048,896]{1,0:T(8,128)(2,1)}) %all-gather.5.cloned.1.call-update) | async-done | bytes 3670032 | tf_op jit(solution)/shard_map/all_gather | solution.py:22
  85.1 0.0 all-gather.7.cloned.1.call-update
  85.1 0.0 all-gather.11.cloned.1.call-start
  85.2 72.9 %all-gather.9.cloned.1.call-done = bf16[2048,896]{1,0:T(8,128)(2,1)} async-done(((bf16[128,896]{1,0:T(8,128)(2,1)}), bf16[2048,896]{1,0:T(8,128)(2,1)}) %all-gather.9.cloned.1.call-update) | async-done | bytes 3670032 | tf_op jit(solution)/shard_map/all_gather | solution.py:22
  158.1 0.0 all-gather.11.cloned.1.call-update
  158.1 0.0 reduce-scatter.7.cloned.1.call-start
  158.1 18.3 %all-gather.7.cloned.1.call-done = bf16[2048,1792]{1,0:T(8,128)(2,1)} async-done(((bf16[2048,896]{1,0:T(8,128)(2,1)}), bf16[2048,1792]{1,0:T(8,128)(2,1)}) %all-gather.7.cloned.1.call-update) | async-done | bytes 7340048 | tf_op jit(solution)/shard_map/all_gather | solution.py:23
  176.4 5.7 %fusion.5 = f32[2048,296]{0,1:T(8,128)S(1)} fusion(bf16[2048,1792]{1,0:T(8,128)(2,1)} %all-gather.7.cloned.1.call-done, bf16[296,1792]{1,0:T(8,128)(2,1)} %param.9), kind=kOutput, calls=%fused_computation.10 | convolution fusion | flops 2172649472 | bytes 10825728 | tf_op jit(solution)/shard_map/dot_general | solution.py:14
  182.1 15.1 %all-gather.11.cloned.1.call-done = bf16[2048,1792]{1,0:T(8,128)(2,1)} async-done(((bf16[2048,896]{1,0:T(8,128)(2,1)}), bf16[2048,1792]{1,0:T(8,128)(2,1)}) %all-gather.11.cloned.1.call-update) | async-done | bytes 7340048 | tf_op jit(solution)/shard_map/all_gather | solution.py:23
  197.2 0.0 copy-done
  197.2 5.6 %fusion.6 = f32[2048,296]{0,1:T(8,128)S(1)} fusion(bf16[2048,1792]{1,0:T(8,128)(2,1)} %all-gather.11.cloned.1.call-done, bf16[296,1792]{1,0:T(8,128)(2,1)S(1)} %copy-done), kind=kOutput, calls=%fused_computation.11 | convolution fusion | flops 2172649472 | bytes 10825728 | tf_op jit(solution)/shard_map/dot_general | solution.py:14
  202.9 0.0 copy-done.4
  202.9 0.0 copy-done.5
  202.9 2.8 fusion.2
  205.7 0.0 copy-start.2
  205.7 7.4 %fusion.7 = f32[2048,1792]{1,0:T(8,128)} fusion(bf16[2048,296]{0,1:T(8,128)(2,1)S(1)} %fusion.2, bf16[296,1792]{1,0:T(8,128)(2,1)S(1)} %copy-done), kind=kOutput, calls=%fused_computation.12 | convolution fusion | flops 2172649472 | bytes 16953344 | tf_op jit(solution)/shard_map/dot_general | solution.py:34
  213.1 9.3 %add_convert_fusion = bf16[2048,1792]{1,0:T(8,128)(2,1)} fusion(f32[2048,1792]{1,0:T(8,128)} %fusion.7, bf16[296,1792]{1,0:T(8,128)(2,1)S(1)} %copy-done.4, f32[2048,296]{0,1:T(8,128)S(1)} %fusion.5, f32[2048,296]{0,1:T(8,128)S(1)} %fusion.6), kind=kOutput, calls=%fused_computation | convolution fusion | flops 2183626752 | bytes 27930624 | tf_op jit(solution)/shard_map/dot_general | solution.py:35
  222.4 10.5 %copy.7 = bf16[2048,1792]{0,1:T(8,128)(2,1)} copy(bf16[2048,1792]{1,0:T(8,128)(2,1)} %add_convert_fusion) | data formatting | bytes 14680064
  232.9 0.0 reduce-scatter.7.cloned.1.call-update
  232.9 0.0 reduce-scatter.5.cloned.1.call-start
  233.0 17.4 %reduce-scatter.7.cloned.1.call-done = bf16[896,2048]{1,0:T(8,128)(2,1)} async-done(((bf16[1792,2048]{1,0:T(8,128)(2,1)}), bf16[896,2048]{1,0:T(8,128)(2,1)}) %reduce-scatter.7.cloned.1.call-update) | async-done | bytes 3670032
  250.4 6.1 %copy.8 = bf16[2048,896]{1,0:T(8,128)(2,1)} copy(bf16[2048,896]{0,1:T(8,128)(2,1)} %bitcast.14) | data formatting | bytes 7340032
  256.5 0.0 reduce-scatter.5.cloned.1.call-update
  256.5 1.3 copy-done.3
  257.8 6.5 %convolution_convert_fusion = bf16[296,1792]{1,0:T(8,128)(2,1)} fusion(bf16[2048,296]{0,1:T(8,128)(2,1)S(1)} %copy-done.3, bf16[2048,1792]{1,0:T(8,128)(2,1)} %all-gather.11.cloned.1.call-done), kind=kOutput, calls=%fused_computation.5 | convolution fusion | flops 2173179904 | bytes 9613312 | tf_op jit(solution)/shard_map/dot_general | solution.py:8
  264.3 79.3 %reduce-scatter.5.cloned.1.call-done = bf16[128,896]{1,0:T(8,128)(2,1)} async-done(((bf16[2048,896]{1,0:T(8,128)(2,1)}), bf16[128,896]{1,0:T(8,128)(2,1)}) %reduce-scatter.5.cloned.1.call-update) | async-done | bytes 229392 | tf_op jit(solution)/shard_map/reduce_scatter | solution.py:37
  (6 shorter events, 0.0 us)
Async XLA Ops:
  7.2 190.1 %copy-start = (bf16[296,1792]{1,0:T(8,128)(2,1)S(1)}, bf16[296,1792]{1,0:T(8,128)(2,1)}, u32[]{:S(2)}) copy-start(bf16[296,1792]{1,0:T(8,128)(2,1)} %param.7) | copy-start | bytes 3182596
  7.2 77.9 %all-gather.5.cloned.1.call-start = ((), (), s32[]{:S(2)}) async-start(), calls=%async_computation.2 | async-start | bytes 3899392 | tf_op jit(solution)/shard_map/all_gather | solution.py:22
  7.9 150.2 %all-gather.9.cloned.1.call-start = ((), (), s32[]{:S(2)}) async-start(), calls=%async_computation.4 | async-start | bytes 3899392 | tf_op jit(solution)/shard_map/all_gather | solution.py:22
  8.7 167.7 %all-gather.7.cloned.1.call-start = ((), (), s32[]{:S(2)}) async-start(), calls=%async_computation.3 | async-start | bytes 11010048 | tf_op jit(solution)/shard_map/all_gather | solution.py:23
  85.1 112.1 %all-gather.11.cloned.1.call-start = ((), (), s32[]{:S(2)}) async-start(), calls=%async_computation.5 | async-start | bytes 11010048 | tf_op jit(solution)/shard_map/all_gather | solution.py:23
  158.1 92.3 %reduce-scatter.7.cloned.1.call-start = ((), (), s32[]{:S(2)}) async-start(), calls=%async_computation.7 | async-start | bytes 11010048
  197.2 5.6 %copy-start.4 = (bf16[296,1792]{1,0:T(8,128)(2,1)S(1)}, bf16[296,1792]{1,0:T(8,128)(2,1)}, u32[]{:S(2)}) copy-start(bf16[296,1792]{1,0:T(8,128)(2,1)} %param.8) | copy-start | bytes 3182596
  197.2 5.6 %copy-start.5 = (bf16[2048,1792]{1,0:T(8,128)(2,1)S(1)}, bf16[2048,1792]{1,0:T(8,128)(2,1)}, u32[]{:S(2)}) copy-start(bf16[2048,1792]{1,0:T(8,128)(2,1)} %all-gather.11.cloned.1.call-done) | copy-start | bytes 22020100
  205.7 7.4 %copy-start.2 = (bf16[2048,296]{0,1:T(8,128)(2,1)}, bf16[2048,296]{0,1:T(8,128)(2,1)S(1)}, u32[]{:S(2)}) copy-start(bf16[2048,296]{0,1:T(8,128)(2,1)S(1)} %fusion.2) | copy-start | bytes 3637252
  232.9 110.7 %reduce-scatter.5.cloned.1.call-start = ((), (), s32[]{:S(2)}) async-start(), calls=%async_computation.6 | async-start | bytes 3899392 | tf_op jit(solution)/shard_map/reduce_scatter | solution.py:37
  256.5 1.3 copy-start.3
  257.8 85.9 %copy-start.1 = (bf16[296,1792]{1,0:T(8,128)(2,1)S(1)}, bf16[296,1792]{1,0:T(8,128)(2,1)}, u32[]{:S(2)}) copy-start(bf16[296,1792]{1,0:T(8,128)(2,1)} %param.7) | copy-start | bytes 3182596
Sparse Core Ops, SparseCore 0:
  10.7 74.3 all-gather.4
  87.9 70.1 all-gather.8
  159.6 16.7 all-gather.6
  177.8 19.3 all-gather.10
  233.0 17.3 reduce-scatter.6
  256.6 86.9 reduce-scatter.4
where the time goes:
time: 351 us; the launch traced here: 350 us
  waiting for transfers between devices  281 us (80%)
  matrix products  37.3 us (11%)
  local copies, waits for them, and re-layouts  17.9 us (5%)
  between operations  14.2 us (4%)
    all_gather x2, waiting for transfers between devices, tokens(): rows = lax.all_gather(block, 'dp', axis=0, tiled=True)  149 us
    reduce_scatter x1, waiting for transfers between devices, per_device(): lax.psum_scatter(partial, 'dp', scatter_dimension=0, tiled=True)  79.3 us
    all_gather x2, waiting for transfers between devices, tokens(): return lax.all_gather(rows, 'mp', axis=1, tiled=True)  33.4 us
    unnamed x7, waiting for transfers between devices  18.9 us
    unnamed x14, local copies, waits for them, and re-layouts  17.9 us
    dot_general x3, matrix products, rdot(): lax.dot_general(left, right, (((1,), (1,)), ((), ())), preferred_element_...  14.2 us
    dot_general x1, matrix products, per_device(): jnp.dot(dup, up_weight, preferred_element_type=jnp.float32)  9.27 us
    dot_general x1, matrix products, per_device(): partial = jnp.dot(dgate, gate_weight, preferred_element_type=jnp.float32)  7.38 us
  transfers between devices with their start and end apart: 6, of which 6 were waited for; matrix products, arithmetic and copies ran while one was open for 3% of the time, Pallas kernels for 0%

commit v1 on v0

--- a/solution.py
+++ b/solution.py
@@ -20,7 +20,7 @@
 
     def tokens(block):
         rows = lax.all_gather(block, "dp", axis=0, tiled=True)
-        return lax.all_gather(rows, "mp", axis=1, tiled=True)
+        return jnp.concatenate(lax.all_gather(rows, "mp"), axis=1)
 
     full_in = tokens(inputs)
     full_cot = tokens(cotangent)

time: 351 us -> 366 us (1.043)
  local copies, waits for them, and re-layouts: 17.9 us -> 39.3 us
  waiting for transfers between devices: 281 us -> 277 us
    reshape x0 -> x2, local copies, waits for them, and re-layouts: none -> 22.7 us  [tokens(): return jnp.concatenate(lax.all_gather(rows, 'mp'), axis=1)]
    all_gather x2, waiting for transfers between devices: 33.4 us -> 27.9 us  [tokens(): return jnp.concatenate(lax.all_gather(rows, 'mp'), axis=1)]
    unnamed x14 -> x12, local copies, waits for them, and re-layouts: 17.9 us -> 16.6 us
  transfers between devices with their start and end apart: 6 -> 6, of which waited for: 6 -> 6; matrix products, arithmetic and copies ran while one was open for 3% -> 5% of each run, Pallas kernels for 0% -> 0%
where the time goes in v1:
time: 366 us; the launch traced here: 365 us
  waiting for transfers between devices  277 us (76%)
  local copies, waits for them, and re-layouts  39.3 us (11%)
  matrix products  34.6 us (9%)
  between operations  14.2 us (4%)
    all_gather x2, waiting for transfers between devices, tokens(): rows = lax.all_gather(block, 'dp', axis=0, tiled=True)  149 us
    reduce_scatter x1, waiting for transfers between devices, per_device(): lax.psum_scatter(partial, 'dp', scatter_dimension=0, tiled=True)  80.5 us
    all_gather x2, waiting for transfers between devices, tokens(): return jnp.concatenate(lax.all_gather(rows, 'mp'), axis=1)  27.9 us
    reshape x2, local copies, waits for them, and re-layouts, tokens(): return jnp.concatenate(lax.all_gather(rows, 'mp'), axis=1)  22.7 us
    unnamed x7, waiting for transfers between devices  18.8 us
    unnamed x12, local copies, waits for them, and re-layouts  16.6 us
    dot_general x3, matrix products, rdot(): lax.dot_general(left, right, (((1,), (1,)), ((), ())), preferred_element_...  11.3 us
    dot_general x1, matrix products, per_device(): jnp.dot(dup, up_weight, preferred_element_type=jnp.float32)  9.28 us
  transfers between devices with their start and end apart: 6, of which 6 were waited for; matrix products, arithmetic and copies ran while one was open for 5% of the time, Pallas kernels for 0%

profile of v1, /device:TPU:0, one launch (start us, length us, event | category | flops | bytes accessed | tf_op | source)
XLA Modules:
  0.0 364.9 jit_solution(13433581957209039403)
XLA Ops:
  7.2 0.0 copy-start
  7.2 0.0 all-gather.9.cloned.1.call-start
  7.2 0.7 all-gather.9.cloned.1.call-update
  7.9 0.0 all-gather.7.cloned.1.call-start
  8.0 0.7 all-gather.7.cloned.1.call-update
  8.7 0.0 all-gather.13.cloned.1.call-start
  8.7 76.4 %all-gather.9.cloned.1.call-done = bf16[2048,896]{1,0:T(8,128)(2,1)} async-done(((bf16[128,896]{1,0:T(8,128)(2,1)}), bf16[2048,896]{1,0:T(8,128)(2,1)}) %all-gather.9.cloned.1.call-update) | async-done | bytes 3670032 | tf_op jit(solution)/shard_map/all_gather | solution.py:22
  85.1 0.0 all-gather.13.cloned.1.call-update
  85.1 0.0 all-gather.11.cloned.1.call-start
  85.2 72.9 %all-gather.7.cloned.1.call-done = bf16[2048,896]{1,0:T(8,128)(2,1)} async-done(((bf16[128,896]{1,0:T(8,128)(2,1)}), bf16[2048,896]{1,0:T(8,128)(2,1)}) %all-gather.7.cloned.1.call-update) | async-done | bytes 3670032 | tf_op jit(solution)/shard_map/all_gather | solution.py:22
  158.1 0.0 all-gather.11.cloned.1.call-update
  158.1 0.0 reduce-scatter.7.cloned.1.call-start
  158.1 18.3 %all-gather.13.cloned.1.call-done = bf16[4096,896]{1,0:T(8,128)(2,1)} async-done(((bf16[2048,896]{1,0:T(8,128)(2,1)}), bf16[4096,896]{1,0:T(8,128)(2,1)}) %all-gather.13.cloned.1.call-update) | async-done | bytes 7340048 | tf_op jit(solution)/shard_map/all_gather | solution.py:23
  176.5 11.3 %copy.10 = bf16[2048,2,896]{0,2,1:T(8,128)(2,1)} copy(bf16[2048,2,896]{2,0,1:T(8,128)(2,1)} %bitcast.25) | data formatting | bytes 14680064 | tf_op jit(solution)/shard_map/reshape | solution.py:23
  187.8 9.6 %all-gather.11.cloned.1.call-done = bf16[4096,896]{1,0:T(8,128)(2,1)} async-done(((bf16[2048,896]{1,0:T(8,128)(2,1)}), bf16[4096,896]{1,0:T(8,128)(2,1)}) %all-gather.11.cloned.1.call-update) | async-done | bytes 7340048 | tf_op jit(solution)/shard_map/all_gather | solution.py:23
  197.4 11.4 %copy.9 = bf16[2048,2,896]{0,2,1:T(8,128)(2,1)} copy(bf16[2048,2,896]{2,0,1:T(8,128)(2,1)} %bitcast.26) | data formatting | bytes 14680064 | tf_op jit(solution)/shard_map/reshape | solution.py:23
  208.8 0.0 copy-done.4
  208.8 5.7 %fusion.5 = f32[2048,296]{0,1:T(8,128)S(1)} fusion(bf16[2048,1792]{0,1:T(8,128)(2,1)} %bitcast.27, bf16[296,1792]{1,0:T(8,128)(2,1)S(1)} %copy-done.4), kind=kOutput, calls=%fused_computation.10 | convolution fusion | flops 2172649472 | bytes 10825728 | tf_op jit(solution)/shard_map/dot_general | solution.py:14
  214.5 0.0 copy-start.3
  214.5 2.4 fusion.6
  216.9 3.2 fusion.2
  220.1 7.4 %fusion.7 = f32[2048,1792]{1,0:T(8,128)} fusion(bf16[2048,296]{0,1:T(8,128)(2,1)S(1)} %fusion.2, bf16[296,1792]{1,0:T(8,128)(2,1)S(1)} %copy-done), kind=kOutput, calls=%fused_computation.12 | convolution fusion | flops 2172649472 | bytes 16953344 | tf_op jit(solution)/shard_map/dot_general | solution.py:34
  227.5 9.3 %add_convert_fusion = bf16[2048,1792]{1,0:T(8,128)(2,1)} fusion(f32[2048,1792]{1,0:T(8,128)} %fusion.7, bf16[296,1792]{1,0:T(8,128)(2,1)S(1)} %copy-done.3, f32[2048,296]{0,1:T(8,128)S(1)} %fusion.5, f32[2048,296]{0,1:T(8,128)S(1)} %fusion.6), kind=kOutput, calls=%fused_computation | convolution fusion | flops 2183626752 | bytes 27930624 | tf_op jit(solution)/shard_map/dot_general | solution.py:35
  236.8 10.5 %copy.11 = bf16[2048,1792]{0,1:T(8,128)(2,1)} copy(bf16[2048,1792]{1,0:T(8,128)(2,1)} %add_convert_fusion) | data formatting | bytes 14680064
  247.3 0.0 reduce-scatter.7.cloned.1.call-update
  247.3 0.0 reduce-scatter.5.cloned.1.call-start
  247.4 17.4 %reduce-scatter.7.cloned.1.call-done = bf16[896,2048]{1,0:T(8,128)(2,1)} async-done(((bf16[1792,2048]{1,0:T(8,128)(2,1)}), bf16[896,2048]{1,0:T(8,128)(2,1)}) %reduce-scatter.7.cloned.1.call-update) | async-done | bytes 3670032
  264.7 6.1 %copy.12 = bf16[2048,896]{1,0:T(8,128)(2,1)} copy(bf16[2048,896]{0,1:T(8,128)(2,1)} %bitcast.28) | data formatting | bytes 7340032
  270.8 0.0 reduce-scatter.5.cloned.1.call-update
  270.9 0.0 copy-start.1
  270.9 6.6 %convolution_convert_fusion = bf16[296,1792]{1,0:T(8,128)(2,1)} fusion(bf16[2048,296]{0,1:T(8,128)(2,1)S(1)} %fusion.2, bf16[2048,1792]{0,1:T(8,128)(2,1)} %bitcast.22), kind=kOutput, calls=%fused_computation.5 | convolution fusion | flops 2173179904 | bytes 9613312 | tf_op jit(solution)/shard_map/dot_general | solution.py:8
  277.5 80.5 %reduce-scatter.5.cloned.1.call-done = bf16[128,896]{1,0:T(8,128)(2,1)} async-done(((bf16[2048,896]{1,0:T(8,128)(2,1)}), bf16[128,896]{1,0:T(8,128)(2,1)}) %reduce-scatter.5.cloned.1.call-update) | async-done | bytes 229392 | tf_op jit(solution)/shard_map/reduce_scatter | solution.py:37
  (6 shorter events, 0.0 us)
Async XLA Ops:
  7.2 207.3 %copy-start = (bf16[296,1792]{1,0:T(8,128)(2,1)S(1)}, bf16[296,1792]{1,0:T(8,128)(2,1)}, u32[]{:S(2)}) copy-start(bf16[296,1792]{1,0:T(8,128)(2,1)} %param.7) | copy-start | bytes 3182596
  7.2 77.9 %all-gather.9.cloned.1.call-start = ((), (), s32[]{:S(2)}) async-start(), calls=%async_computation.3 | async-start | bytes 3899392 | tf_op jit(solution)/shard_map/all_gather | solution.py:22
  7.9 150.2 %all-gather.7.cloned.1.call-start = ((), (), s32[]{:S(2)}) async-start(), calls=%async_computation.2 | async-start | bytes 3899392 | tf_op jit(solution)/shard_map/all_gather | solution.py:22
  8.7 167.8 %all-gather.13.cloned.1.call-start = ((), (), s32[]{:S(2)}) async-start(), calls=%async_computation.6 | async-start | bytes 11010048 | tf_op jit(solution)/shard_map/all_gather | solution.py:23
  85.1 112.2 %all-gather.11.cloned.1.call-start = ((), (), s32[]{:S(2)}) async-start(), calls=%async_computation.5 | async-start | bytes 11010048 | tf_op jit(solution)/shard_map/all_gather | solution.py:23
  158.1 106.7 %reduce-scatter.7.cloned.1.call-start = ((), (), s32[]{:S(2)}) async-start(), calls=%async_computation.7 | async-start | bytes 11010048
  197.4 11.4 %copy-start.4 = (bf16[296,1792]{1,0:T(8,128)(2,1)S(1)}, bf16[296,1792]{1,0:T(8,128)(2,1)}, u32[]{:S(2)}) copy-start(bf16[296,1792]{1,0:T(8,128)(2,1)} %param.9) | copy-start | bytes 3182596
  208.8 5.7 %copy-start.2 = (bf16[2048,2,896]{0,2,1:T(8,128)(2,1)S(1)}, bf16[2048,2,896]{0,2,1:T(8,128)(2,1)}, u32[]{:S(2)}) copy-start(bf16[2048,2,896]{0,2,1:T(8,128)(2,1)} %copy.10) | copy-start | bytes 22020100
  214.5 2.5 copy-start.3
  247.3 110.7 %reduce-scatter.5.cloned.1.call-start = ((), (), s32[]{:S(2)}) async-start(), calls=%async_computation.4 | async-start | bytes 3899392 | tf_op jit(solution)/shard_map/reduce_scatter | solution.py:37
  270.9 87.2 %copy-start.1 = (bf16[296,1792]{1,0:T(8,128)(2,1)S(1)}, bf16[296,1792]{1,0:T(8,128)(2,1)}, u32[]{:S(2)}) copy-start(bf16[296,1792]{1,0:T(8,128)(2,1)} %param.7) | copy-start | bytes 3182596
Sparse Core Ops, SparseCore 0:
  10.7 74.3 all-gather.8
  87.9 70.1 all-gather.6
  159.6 16.8 all-gather.12
  177.9 19.4 all-gather.10
  247.4 17.2 reduce-scatter.6
  271.0 86.9 reduce-scatter.4
